TPU v7x, 32 devices: a whole 2x2x4 slice. The times are simulated.
32 devices in a mesh: grp: 8 (over z, core), sib: 4 (over y, x).
Axes of the slice: x: 2, y: 2, z: 4, core: 2. Of those that a mesh axis runs over, the one named last changes fastest.
Arguments:
- targets: float32 [40960, 256], P(('grp', 'sib')), may hold values from -6 to 6
- leaf_order: int32 [32, 1280], P(('grp', 'sib')), may hold values from 0 to 1279, each once within a row
- near_block: float32 [40960, 1280], P(('grp', 'sib')), may hold values from -0.15625 to 0.15625
- leaf_basis: float32 [40960, 128], P(('grp', 'sib')), may hold values from -0.15625 to 0.15625
- sibling_coupling: float32 [4096, 512], P(('grp', 'sib')), may hold values from -0.5 to 0.5
- transfer: float32 [4096, 128], P(('grp', 'sib')), may hold values from -0.5 to 0.5
- top_coupling: float32 [1024, 1024], P('grp', 'sib'), may hold values from -0.1875 to 0.1875
Outputs:
- coefficients: float32 [40960, 256], P(('grp', 'sib'))
- fitted: float32 [40960, 256], P(('grp', 'sib'))
Inputs may be any that keep to these rules, and one draw needn't show every extreme that they name: `leaf_order`: each row of 1280 entries holds every number of 0 to 1279 once.
All inputs are finite; a program needn't handle non-finite values.
Results may differ from a plain program's by a relative error of at most 0.00025.
Values sent between devices are 32-bit elements; how exact they have to be, the bound alone decides.
A program may use at most 64 MiB of HBM per device.

v0:
```python
import jax
import jax.numpy as jnp
from jax import lax
from jax.sharding import PartitionSpec as P

ITERS = 3


step_size = 0.5
shrink_rate = 0.1
highest_level = lax.Precision.HIGHEST


def matmul(left, right):
    return jnp.dot(left, right, precision=highest_level, preferred_element_type=jnp.float32)


def shards(targets, leaf_order, near_block, leaf_basis, sibling_coupling, transfer, top_coupling):
    ordering = leaf_order[0]
    tree_targets = jnp.take(targets, ordering, axis=0)
    basis_rank = transfer.shape[0]
    sib_index = lax.axis_index("sib")
    grp_index = lax.axis_index("grp")
    block_owner = jnp.arange(sibling_coupling.shape[1]) // basis_rank
    sibling_row = jnp.where((block_owner == sib_index)[None, :], 0.0, sibling_coupling)
    top_whole = lax.all_gather(top_coupling, "sib", axis=1, tiled=True)
    group_owner = jnp.arange(top_whole.shape[1]) // basis_rank
    top_row = jnp.where((group_owner == grp_index)[None, :], 0.0, top_whole)
    transfer_all = lax.all_gather(transfer, "sib", axis=0, tiled=True)
    weight_coefficients = step_size * tree_targets
    fitted = weight_coefficients
    for iteration in range(ITERS):
        leaf_coefficients = matmul(leaf_basis.T, weight_coefficients)
        both_block_rows = lax.all_gather(leaf_coefficients, "sib", axis=0, tiled=True)
        sibling_sum = matmul(sibling_row, both_block_rows)
        cluster_coefficient = matmul(transfer_all.T, both_block_rows)
        stacked = lax.all_gather(cluster_coefficient, "grp", axis=0, tiled=True)
        root_sum = matmul(top_row, stacked)
        downward_pass = sibling_sum + matmul(transfer, root_sum)
        fitted = jnp.tanh(
            matmul(near_block, weight_coefficients) + matmul(leaf_basis, downward_pass)
        )
        weight_coefficients = (
            weight_coefficients
            + step_size * (tree_targets - fitted)
            - step_size * shrink_rate * weight_coefficients
        )
    coeffs_out = jnp.zeros_like(weight_coefficients).at[ordering].set(weight_coefficients)
    fitted_out = jnp.zeros_like(fitted).at[ordering].set(fitted)
    return (coeffs_out, fitted_out)


def solution(mesh):
    return jax.shard_map(
        shards,
        mesh=mesh,
        in_specs=(
            P(("grp", "sib"), None),
            P(("grp", "sib"), None),
            P(("grp", "sib"), None),
            P(("grp", "sib"), None),
            P(("grp", "sib"), None),
            P(("grp", "sib"), None),
            P("grp", "sib"),
        ),
        out_specs=(P(("grp", "sib"), None), P(("grp", "sib"), None)),
        check_vma=False,
    )
```

profile of v0, /device:TPU:0, one launch (start us, length us, event | category | flops | bytes accessed | tf_op | source)
XLA Modules:
  0.0 197.5 jit_solution(15285919574683306363)
XLA Ops:
  7.2 0.0 copy-start
  7.2 0.0 all-gather.4.cloned.1.call-start
  7.2 0.8 fusion.54
  8.0 0.7 reduce.1
  8.8 10.8 %all_gather.26 = f32[512,128]{1,0:T(8,128)S(1)} all-gather(f32[128,128]{1,0:T(8,128)} %param.12), channel_id=1, replica_groups=mesh['grp'=8,'sib'=4] {'sib'}, dimensions={0}, use_global_device_ids=true | all-gather | bytes 327680 | tf_op jit(solution)/shard_map/all_gather | solution.py:29
  19.5 0.0 copy-done
  19.5 4.1 %gather_fusion = f32[1280,256]{1,0:T(8,128)} fusion(f32[1280,256]{1,0:T(8,128)S(1)} %copy-done, s32[2048]{0:T(1024)S(1)} %pad_clamp_fusion), kind=kCustom, calls=%fused_computation | custom fusion | bytes 2626560 | tf_op jit(solution)/shard_map/jit(_take)/gather | solution.py:20
  23.6 0.0 copy-start.1
  23.6 1.8 copy.11
  25.4 0.0 copy-done.1
  25.4 1.2 fusion.18
  26.7 11.8 %all_gather.24 = f32[512,256]{0,1:T(8,128)S(1)} all-gather(f32[128,256]{0,1:T(8,128)S(1)} %fusion.18), channel_id=1, replica_groups=mesh['grp'=8,'sib'=4] {'sib'}, dimensions={0}, use_global_device_ids=true | all-gather | bytes 655360 | tf_op jit(solution)/shard_map/all_gather | solution.py:34
  38.5 0.8 copy-done.10
  39.3 1.2 convolution_bitcast_fusion.2
  40.5 0.0 all-gather.4.cloned.1.call-update
  40.5 0.0 all-gather.6.cloned.1.call-start
  40.6 11.0 %all_gather.25 = f32[128,1024]{1,0:T(8,128)} all-gather(f32[128,256]{1,0:T(8,128)} %param.13), channel_id=1, replica_groups=mesh['grp'=8,'sib'=4] {'sib'}, dimensions={1}, use_global_device_ids=true | all-gather | bytes 655360 | tf_op jit(solution)/shard_map/all_gather | solution.py:26
  51.6 0.6 fusion.59
  52.2 9.6 %fusion.16 = f32[256,1280]{1,0:T(8,128)} fusion(f32[1280,1280]{1,0:T(8,128)} %param.9, f32[1280,256]{0,1:T(8,128)S(1)} %copy.11, pred[1280]{0:T(1024)(128)(4,1)S(1)} %compare_and_fusion), kind=kOutput, calls=%fused_computation.23 | convolution fusion | flops 5033820160 | bytes 9176320 | tf_op jit(solution)/shard_map/dot_general | solution.py:15
  61.8 3.1 %all-gather.4.cloned.1.call-done = f32[1024,256]{0,1:T(8,128)} async-done(((f32[128,256]{0,1:T(8,128)}), f32[1024,256]{0,1:T(8,128)}) %all-gather.4.cloned.1.call-update) | async-done | bytes 1048592 | tf_op jit(solution)/shard_map/all_gather | solution.py:37
  64.9 2.7 %fusion.37 = f32[128,256]{1,0:T(8,128)S(1)} fusion(f32[1024,256]{0,1:T(8,128)} %all-gather.4.cloned.1.call-done, f32[128,1024]{1,0:T(8,128)} %all_gather.25, pred[1024]{0:T(1024)(128)(4,1)S(1)} %fusion.55), kind=kOutput, calls=%fused_computation.53 | convolution fusion | flops 402784256 | bytes 1704960 | tf_op jit(solution)/shard_map/dot_general | solution.py:15
  67.5 1.1 convolution_bitcast_fusion.5
  68.7 0.0 copy-done.11
  68.7 0.0 copy-done.15
  68.7 1.6 convolution_add_fusion.5
  70.3 0.0 copy-done.8
  70.3 1.5 fusion.5
  71.8 0.0 copy-start.4
  71.8 1.2 convolution_bitcast_fusion.7
  73.0 13.5 %all_gather.28 = f32[512,256]{0,1:T(8,128)S(1)} all-gather(f32[128,256]{0,1:T(8,128)S(1)} %convolution_bitcast_fusion.7), channel_id=1, replica_groups=mesh['grp'=8,'sib'=4] {'sib'}, dimensions={0}, use_global_device_ids=true | all-gather | bytes 655360 | tf_op jit(solution)/shard_map/all_gather | solution.py:34
  86.5 0.0 copy-done.4
  86.5 0.8 copy-done.13
  87.3 1.2 convolution_bitcast_fusion.1
  88.5 0.0 all-gather.6.cloned.1.call-update
  88.6 0.6 all-gather.8.cloned.1.call-start
  89.1 9.9 %fusion.73 = f32[256,1280]{1,0:T(8,128)} fusion(f32[1280,256]{0,1:T(8,128)} %copy-done.4, f32[1280,1280]{1,0:T(8,128)} %param.9), kind=kOutput, calls=%fused_computation.101 | convolution fusion | flops 5033164800 | bytes 9175040 | tf_op jit(solution)/shard_map/dot_general | solution.py:15
  99.1 12.4 %all-gather.6.cloned.1.call-done = f32[1024,256]{0,1:T(8,128)} async-done(((f32[128,256]{0,1:T(8,128)}), f32[1024,256]{0,1:T(8,128)}) %all-gather.6.cloned.1.call-update) | async-done | bytes 1048592 | tf_op jit(solution)/shard_map/all_gather | solution.py:37
  111.5 2.7 %fusion.35 = f32[128,256]{1,0:T(8,128)S(1)} fusion(f32[1024,256]{0,1:T(8,128)} %all-gather.6.cloned.1.call-done, f32[128,1024]{1,0:T(8,128)} %all_gather.25, pred[1024]{0:T(1024)(128)(4,1)S(1)} %fusion.55), kind=kOutput, calls=%fused_computation.51 | convolution fusion | flops 402784256 | bytes 1704960 | tf_op jit(solution)/shard_map/dot_general | solution.py:15
  114.1 1.1 convolution_bitcast_fusion.4
  115.3 1.8 convolution_add_fusion.4
  117.1 0.0 copy-done.5
  117.1 0.0 copy-done.7
  117.1 1.5 fusion.11
  118.6 0.0 copy-start.2
  118.6 1.2 convolution_bitcast_fusion.6
  119.8 13.7 %all_gather.30 = f32[512,256]{0,1:T(8,128)S(1)} all-gather(f32[128,256]{0,1:T(8,128)S(1)} %convolution_bitcast_fusion.6), channel_id=1, replica_groups=mesh['grp'=8,'sib'=4] {'sib'}, dimensions={0}, use_global_device_ids=true | all-gather | bytes 655360 | tf_op jit(solution)/shard_map/all_gather | solution.py:34
  133.5 0.0 copy-done.2
  133.5 0.8 copy-done.12
  134.3 1.2 convolution_bitcast_fusion
  135.6 0.0 all-gather.8.cloned.1.call-update
  135.6 9.9 %fusion.74 = f32[256,1280]{1,0:T(8,128)} fusion(f32[1280,256]{0,1:T(8,128)} %copy-done.2, f32[1280,1280]{1,0:T(8,128)} %param.9), kind=kOutput, calls=%fused_computation.102 | convolution fusion | flops 5033164800 | bytes 9175040 | tf_op jit(solution)/shard_map/dot_general | solution.py:15
  145.5 13.0 %all-gather.8.cloned.1.call-done = f32[1024,256]{0,1:T(8,128)} async-done(((f32[128,256]{0,1:T(8,128)}), f32[1024,256]{0,1:T(8,128)}) %all-gather.8.cloned.1.call-update) | async-done | bytes 1048592 | tf_op jit(solution)/shard_map/all_gather | solution.py:37
  158.5 2.7 %fusion.33 = f32[128,256]{1,0:T(8,128)S(1)} fusion(f32[1024,256]{0,1:T(8,128)} %all-gather.8.cloned.1.call-done, f32[128,1024]{1,0:T(8,128)} %all_gather.25, pred[1024]{0:T(1024)(128)(4,1)S(1)} %fusion.55), kind=kOutput, calls=%fused_computation.49 | convolution fusion | flops 402784256 | bytes 1704960 | tf_op jit(solution)/shard_map/dot_general | solution.py:15
  161.2 1.1 convolution_bitcast_fusion.3
  162.3 0.0 copy-done.14
  162.3 1.7 convolution_add_fusion.3
  164.0 0.0 copy-done.3
  164.0 0.0 copy-done.6
  164.0 3.0 %multiply_subtract_fusion = (f32[1280,256]{0,1:T(8,128)}, f32[1280,256]{0,1:T(8,128)}) fusion(f32[1280,256]{0,1:T(8,128)S(1)} %copy-done.3, f32[1280,256]{0,1:T(8,128)S(1)} %copy.11, pred[1280]{0:T(1024)(128)(4,1)S(1)} %compare_and_fusion, f32[256,1280]{1,0:T(8,128)S(1)} %copy-done.6, f32[128,256]{1,0:T(8,128)S(1)} %convolution_add_fusion.3, ...), kind=kOutput, calls=%fused_computation.20 | convolution fusion | flops 505610240 | bytes 7341312 | tf_op jit(solution)/shard_map/dot_general | solution.py:15
  167.1 2.9 %copy.12 = f32[1280,256]{1,0:T(8,128)} copy(f32[1280,256]{0,1:T(8,128)} %get-tuple-element.2) | data formatting | bytes 2621440 | tf_op jit(solution)/shard_map/sub | solution.py:44
  170.0 0.0 copy-done.9
  170.0 1.5 copy.13
  171.4 9.8 %scatter_custom_fusion = f32[1280,256]{1,0:T(8,128)} fusion(s32[1280]{0:T(1024)S(1)} %fusion.54, f32[1280,256]{1,0:T(8,128)} %copy.12, f32[]{:T(128)} %constant.49.clone.1), kind=kCustom, calls=%fused_computation.45 | custom fusion | bytes 1311232 | tf_op jit(solution)/shard_map/scatter | solution.py:48
  181.2 9.6 %scatter_custom_fusion.1 = f32[1280,256]{1,0:T(8,128)} fusion(s32[1280]{0:T(1024)S(1)} %fusion.54, f32[1280,256]{1,0:T(8,128)} %copy.13, f32[]{:T(128)} %constant.49.clone.1), kind=kCustom, calls=%fused_computation.43 | custom fusion | bytes 1311232 | tf_op jit(solution)/shard_map/scatter | solution.py:49
  (15 shorter events, 0.0 us)
Async XLA Ops:
  7.2 12.4 %copy-start = (f32[1280,256]{1,0:T(8,128)S(1)}, f32[1280,256]{1,0:T(8,128)}, u32[]{:S(2)}) copy-start(f32[1280,256]{1,0:T(8,128)} %param.7) | copy-start | bytes 3932164
  7.2 57.7 %all-gather.4.cloned.1.call-start = ((), (), s32[]{:S(2)}) async-start(), calls=%async_computation | async-start | bytes 1179648 | tf_op jit(solution)/shard_map/all_gather | solution.py:37
  23.6 1.8 copy-start.1
  38.5 0.8 copy-start.10
  40.5 70.9 %all-gather.6.cloned.1.call-start = ((), (), s32[]{:S(2)}) async-start(), calls=%async_computation.1 | async-start | bytes 1179648 | tf_op jit(solution)/shard_map/all_gather | solution.py:37
  64.8 3.8 %copy-start.11 = (f32[512,256]{0,1:T(8,128)S(1)}, f32[512,256]{0,1:T(8,128)}, u32[]{:S(2)}) copy-start(f32[512,256]{0,1:T(8,128)} %copy-done.10) | copy-start | bytes 1572868
  64.9 3.8 %copy-start.15 = (pred[512]{0:T(512)(128)(4,1)S(1)}, pred[512]{0:T(512)(128)(4,1)}, u32[]{:S(2)}) copy-start(pred[512]{0:T(512)(128)(4,1)} %fusion.59) | copy-start | bytes 1540
  64.9 5.4 %copy-start.8 = (f32[256,1280]{1,0:T(8,128)S(1)}, f32[256,1280]{1,0:T(8,128)}, u32[]{:S(2)}) copy-start(f32[256,1280]{1,0:T(8,128)} %fusion.16) | copy-start | bytes 3932164
  71.8 14.7 %copy-start.4 = (f32[1280,256]{0,1:T(8,128)}, f32[1280,256]{0,1:T(8,128)S(1)}, u32[]{:S(2)}) copy-start(f32[1280,256]{0,1:T(8,128)S(1)} %fusion.5) | copy-start | bytes 3932164
  86.5 0.8 copy-start.13
  88.6 69.9 %all-gather.8.cloned.1.call-start = ((), (), s32[]{:S(2)}) async-start(), calls=%async_computation.2 | async-start | bytes 1179648 | tf_op jit(solution)/shard_map/all_gather | solution.py:37
  111.4 5.6 %copy-start.5 = (f32[1280,256]{0,1:T(8,128)S(1)}, f32[1280,256]{0,1:T(8,128)}, u32[]{:S(2)}) copy-start(f32[1280,256]{0,1:T(8,128)} %copy-done.4) | copy-start | bytes 3932164
  111.5 5.6 %copy-start.7 = (f32[256,1280]{1,0:T(8,128)S(1)}, f32[256,1280]{1,0:T(8,128)}, u32[]{:S(2)}) copy-start(f32[256,1280]{1,0:T(8,128)} %fusion.73) | copy-start | bytes 3932164
  118.6 14.9 %copy-start.2 = (f32[1280,256]{0,1:T(8,128)}, f32[1280,256]{0,1:T(8,128)S(1)}, u32[]{:S(2)}) copy-start(f32[1280,256]{0,1:T(8,128)S(1)} %fusion.11) | copy-start | bytes 3932164
  133.5 0.8 copy-start.12
  145.5 16.8 %copy-start.14 = (f32[128,512]{1,0:T(8,128)S(1)}, f32[128,512]{1,0:T(8,128)}, u32[]{:S(2)}) copy-start(f32[128,512]{1,0:T(8,128)} %param.11) | copy-start | bytes 786436
  158.5 5.5 %copy-start.3 = (f32[1280,256]{0,1:T(8,128)S(1)}, f32[1280,256]{0,1:T(8,128)}, u32[]{:S(2)}) copy-start(f32[1280,256]{0,1:T(8,128)} %copy-done.2) | copy-start | bytes 3932164
  158.5 5.5 %copy-start.6 = (f32[256,1280]{1,0:T(8,128)S(1)}, f32[256,1280]{1,0:T(8,128)}, u32[]{:S(2)}) copy-start(f32[256,1280]{1,0:T(8,128)} %fusion.74) | copy-start | bytes 3932164
  167.1 2.9 %copy-start.9 = (f32[1280,256]{0,1:T(8,128)S(1)}, f32[1280,256]{0,1:T(8,128)}, u32[]{:S(2)}) copy-start(f32[1280,256]{0,1:T(8,128)} %get-tuple-element.3) | copy-start | bytes 3932164
Sparse Core Ops, SparseCore 0:
  40.7 24.1 all-gather.3
  88.7 22.7 all-gather.5
  135.7 22.7 all-gather.7
where the time goes:
time: 201 us; the launch traced here: 198 us
  blocking collectives  60.7 us (30%)
  matrix products  59.2 us (29%)
  local copies, waits for them, and re-layouts  32.1 us (16%)
  waiting for transfers between devices  28.5 us (14%)
  between operations  14.2 us (7%)
  other arithmetic  2.14 us (1%)
    dot_general x21, matrix products, matmul(): jnp.dot(left, right, precision=highest_level, preferred_element_type=jnp....  59.2 us
    all_gather x3, blocking collectives, shards(): lax.all_gather(leaf_coefficients, 'sib', axis=0, tiled=True)  39 us
    all_gather x3, waiting for transfers between devices, shards(): stacked = lax.all_gather(cluster_coefficient, 'grp', axis=0, tiled=True)  28.4 us
    all_gather x1, blocking collectives, shards(): top_whole = lax.all_gather(top_coupling, 'sib', axis=1, tiled=True)  11 us
    all_gather x1, blocking collectives, shards(): transfer_all = lax.all_gather(transfer, 'sib', axis=0, tiled=True)  10.8 us
    scatter x1, local copies, waits for them, and re-layouts, shards(): jnp.zeros_like(weight_coefficients).at[ordering].set(weight_coefficients)  9.77 us
    scatter x1, local copies, waits for them, and re-layouts, shards(): fitted_out = jnp.zeros_like(fitted).at[ordering].set(fitted)  9.56 us
    gather x2, local copies, waits for them, and re-layouts, shards(): tree_targets = jnp.take(targets, ordering, axis=0)  5.88 us
  transfers between devices with their start and end apart: 3, of which 3 were waited for; matrix products, arithmetic and copies ran while one was open for 15% of the time, Pallas kernels for 0%

commit v1 on v0

v1 whole, which is shorter than its diff:
```python
import functools

import jax
import jax.numpy as jnp
from jax import lax
from jax.experimental import pallas as pl
from jax.experimental.pallas import tpu as pltpu
from jax.sharding import PartitionSpec as P

ITERS = 3
step_size = 0.5
shrink_rate = 0.1
f32 = jnp.float32
bf16 = jnp.bfloat16
MESH = pl.DeviceIdType.MESH


def split(value):
    high = value.astype(bf16)
    return high, (value - high.astype(f32)).astype(bf16)


def dot(left, right):
    return jnp.dot(left, right, preferred_element_type=f32)


def dot3(left, right):
    return dot(left[0], right[0]) + (dot(left[0], right[1]) + dot(left[1], right[0]))


def kernel(n_grp, n_sib, targets, order, near, basis, sibling, transfer, top,
           prev_out, field_out,
           t_v, o_v, n_v, u_v, s_v, r_v, top_v,
           oc_v, g_v, gt_v, nh_v, nl_v, uh_v, ul_v, wh_v, wl_v, ph_v, pl_v,
           uwh_v, uwl_v, bh_v, bl_v, tt_v, x_v, xh_v, xl_v, pre_v, prev_v,
           c_own, c_all, d_own, d_sib, d_grp, z_all,
           load_sem, out_sem, top_send, top_recv, d_send, d_recv, c_send, c_recv,
           g_send, g_recv, z_send, z_recv):
    leaf, cols = t_v.shape
    rank = r_v.shape[0]
    part = cols // n_sib
    tile = 256 if leaf % 256 == 0 else leaf
    tiles = leaf // tile
    n_chip = n_grp // 2
    grp, sib = lax.axis_index("grp"), lax.axis_index("sib")
    chip, core = lax.div(grp, 2), lax.rem(grp, 2)
    partner = (grp + 1 - 2 * core, sib)

    def sib_at(k):
        return lax.rem(sib + k + n_sib, n_sib)

    def chip_at(k):
        return lax.rem(chip + k + n_chip, n_chip)

    peers = [(grp, sib_at(k)) for k in range(1, n_sib)]
    peers += [(chip_at(k) * 2 + core, sib) for k in range(1, n_chip)] + [partner]
    barrier = pltpu.get_barrier_semaphore()
    for peer in peers:
        pl.semaphore_signal(barrier, inc=1, device_id=peer, device_id_type=MESH)

    loads = [pltpu.make_async_copy(src, dst, load_sem.at[i]) for i, (src, dst) in enumerate((
        (order, o_v), (targets, t_v), (basis, u_v), (transfer, r_v), (near, n_v),
        (sibling, s_v), (top, top_v.at[sib])))]
    for load in loads:
        load.start()
    pending = []

    def send(src, dst, send_sem, recv_sem, peer):
        copy = pltpu.make_async_remote_copy(
            src_ref=src, dst_ref=dst, send_sem=send_sem, recv_sem=recv_sem,
            device_id=peer, device_id_type=MESH)
        copy.start()
        pending.append(copy)
        return copy

    def rows(i):
        return pl.ds(pl.multiple_of(i * tile, tile), tile)

    def over_tiles(first, last, body):
        if last > first:
            pl.loop(first, last)(lambda i: body(rows(i), i))

    loads[0].wait()
    oc_v[...] = jnp.broadcast_to(o_v[...].astype(f32), (128, leaf)).T
    pl.semaphore_wait(barrier, len(peers))
    top_copies = [send(top, top_v.at[sib], top_send.at[k], top_recv.at[k], (grp, sib_at(k)))
                  for k in range(1, n_sib)]
    loads[1].wait()
    loads[2].wait()
    loads[3].wait()

    th, tl = split(t_v[...])
    xh_v[...] = th
    tlow = tl
    prev_v[...] = jnp.zeros_like(prev_v)
    xl_v[...] = tlow

    def to_tree(r, i):
        own = oc_v[r, :]
        for b in range(leaf // 128):
            hit = own == (lax.broadcasted_iota(jnp.int32, (tile, 128), 1) + 128 * b).astype(f32)
            g_v[:, b * 128:(b + 1) * 128] = jnp.where(hit, 1.0, 0.0).astype(bf16)
        tt_v[r, :] = dot(g_v[...], xh_v[...]) + dot(g_v[...], xl_v[...])

    over_tiles(0, tiles, to_tree)

    def start_x(r, i):
        value = step_size * tt_v[r, :]
        x_v[r, :] = value
        xh_v[r, :], xl_v[r, :] = split(value)

    over_tiles(0, tiles, start_x)

    r_pair = split(r_v[...])
    ut = u_v[...].T
    ut_pair = split(ut)
    uwh_v[:rank, :], uwl_v[:rank, :] = ut_pair
    uwh_v[rank:, :], uwl_v[rank:, :] = split(dot3(split(r_v[...].T), ut_pair))

    def second_basis(r, i):
        pair = split(u_v[r, :])
        uh_v[r, :], ul_v[r, :] = pair
        wh_v[r, :], wl_v[r, :] = split(dot3(pair, r_pair))

    def near_first(r, i):
        pair = split(n_v[r, :])
        nh_v[r, :], nl_v[r, :] = pair
        pre_v[r, :] = dot3(pair, (xh_v[...], xl_v[...]))

    def near_again(r, i):
        pre_v[r, :] = dot3((nh_v[r, :], nl_v[r, :]), (xh_v[...], xl_v[...]))

    def to_data(r, i):
        q = lax.broadcasted_iota(jnp.int32, (tile, leaf), 0) + i * tile
        gt_v[r, :] = jnp.where(q == o_v[...], 1.0, 0.0).astype(bf16)
        ph_v[r, :] = dot(gt_v[r, :], wh_v[...]).astype(bf16)
        pl_v[r, :] = dot(gt_v[r, :], wl_v[...]).astype(bf16)

    for it in range(ITERS):
        final = it == ITERS - 1
        both = dot3((uwh_v[...], uwl_v[...]), (xh_v[...], xl_v[...]))
        d_own[it] = both[rank:, :].T
        d_copies = [send(d_own.at[it, pl.ds(pl.multiple_of(sib_at(k) * part, part), part)], d_sib.at[it, k],
                         d_send.at[it, k], d_recv.at[it, k], (grp, sib_at(k))) for k in range(1, n_sib)]
        c_own[it] = both[:rank, :]
        c_copies = [send(c_own.at[it], c_all.at[it, k], c_send.at[it, k], c_recv.at[it, k],
                         (grp, sib_at(k))) for k in range(1, n_sib)]
        if it == 0:
            over_tiles(0, tiles, second_basis)
            loads[4].wait()
        near_part = near_first if it == 0 else near_again
        early = (tiles + 1) // 2 if it == 0 else tiles
        over_tiles(0, early, near_part)

        total = d_own[it, pl.ds(pl.multiple_of(sib * part, part), part), :]
        for k in range(1, n_sib):
            d_copies[k - 1].wait_recv()
            total = total + d_sib[it, k]
        d_grp[it, 0, 0] = total
        mine = d_grp.at[it, 0, 0]
        g_copies = [send(mine, d_grp.at[it, k, 0], g_send.at[it, k, 0], g_recv.at[it, k, 0],
                         (chip_at(k) * 2 + core, sib)) for k in range(1, n_chip)]
        relays = [send(mine, d_grp.at[it, 0, 1], g_send.at[it, 0, 1], g_recv.at[it, 0, 1], partner)]

        over_tiles(early, tiles, near_part)
        if it == 0:
            for copy in top_copies:
                copy.wait_recv()
            loads[5].wait()
            loads[6].wait()
            width = top_v.shape[2]
            for j in range(n_sib):
                bh_v[j * width:(j + 1) * width, :], bl_v[j * width:(j + 1) * width, :] = split(top_v[j].T)
            over_tiles(0, tiles, to_data)
        if final:
            def prev_to_data(r, i):
                prev_v[r, :] = dot(gt_v[r, :], xh_v[...]) + dot(gt_v[r, :], xl_v[...])
            over_tiles(0, tiles, prev_to_data)
            out_prev = pltpu.make_async_copy(prev_v, prev_out, out_sem.at[0])
            out_prev.start()

        def from_group(k, other):
            group = chip_at(-k) * 2 + (1 - core if other else core)
            at = pl.ds(pl.multiple_of(group * rank, rank), rank)
            return dot3(split(d_grp[it, k, other]), (bh_v[at, :], bl_v[at, :]))

        for k in range(1, n_chip):
            g_copies[k - 1].wait_recv()
            relays.append(send(d_grp.at[it, k, 0], d_grp.at[it, k, 1], g_send.at[it, k, 1],
                               g_recv.at[it, k, 1], partner))
        relays[0].wait_recv()
        z_part = from_group(0, 1)
        for k in range(1, n_chip):
            z_part = z_part + from_group(k, 0)
        for k in range(1, n_chip):
            relays[k].wait_recv()
            z_part = z_part + from_group(k, 1)
        here = pl.ds(pl.multiple_of(sib * part, part), part)
        z_all[it, here, :] = z_part
        z_copies = [send(z_all.at[it, here], z_all.at[it, here], z_send.at[it, k], z_recv.at[it, k],
                         (grp, sib_at(k))) for k in range(1, n_sib)]

        down = jnp.zeros((rank, cols), f32)
        for k in range(1, n_sib):
            c_copies[k - 1].wait_recv()
            block = s_v[:, pl.ds(pl.multiple_of(sib_at(-k) * rank, rank), rank)]
            down = down + dot3(split(block), split(c_all[it, k]))
        down_pair = split(down)

        def add_siblings(r, i):
            pre_v[r, :] = pre_v[r, :] + dot3((uh_v[r, :], ul_v[r, :]), down_pair)

        over_tiles(0, tiles, add_siblings)
        if final:
            def pre_split(r, i):
                xh_v[r, :], xl_v[r, :] = split(pre_v[r, :])

            def pre_to_data(r, i):
                pre_v[r, :] = dot(gt_v[r, :], xh_v[...]) + dot(gt_v[r, :], xl_v[...])

            over_tiles(0, tiles, pre_split)
            over_tiles(0, tiles, pre_to_data)

        for copy in z_copies:
            copy.wait_recv()
        z_pair = split(z_all[it].T)
        if final:
            outs = []
            for i in range(tiles):
                r = pl.ds(i * tile, tile)
                pre_v[r, :] = pre_v[r, :] + dot3((ph_v[r, :], pl_v[r, :]), z_pair)
                outs.append(pltpu.make_async_copy(pre_v.at[r], field_out.at[r], out_sem.at[1 + i]))
                outs[-1].start()
        else:
            def update(r, i):
                fitted = jnp.tanh(pre_v[r, :] + dot3((wh_v[r, :], wl_v[r, :]), z_pair))
                old = x_v[r, :]
                new = old + step_size * (tt_v[r, :] - fitted) - step_size * shrink_rate * old
                x_v[r, :] = new
                xh_v[r, :], xl_v[r, :] = split(new)

            over_tiles(0, tiles, update)

    for copy in pending:
        copy.wait_send()
    out_prev.wait()
    for copy in outs:
        copy.wait()


def shards(n_grp, n_sib, targets, leaf_order, near_block, leaf_basis, sibling_coupling, transfer, top_coupling):
    leaf, cols = targets.shape
    rank = transfer.shape[0]
    part = cols // n_sib
    tile = 256 if leaf % 256 == 0 else leaf
    n_chip = n_grp // 2
    dma = pltpu.SemaphoreType.DMA
    vmem = pltpu.VMEM
    previous, field = pl.pallas_call(
        functools.partial(kernel, n_grp, n_sib),
        out_shape=(jax.ShapeDtypeStruct((leaf, cols), f32),) * 2,
        in_specs=[pl.BlockSpec(memory_space=pl.ANY)] * 7,
        out_specs=(pl.BlockSpec(memory_space=pl.ANY),) * 2,
        scratch_shapes=[
            vmem((leaf, cols), f32), vmem((1, leaf), jnp.int32), vmem((leaf, leaf), f32),
            vmem((leaf, rank), f32), vmem(sibling_coupling.shape, f32), vmem((rank, rank), f32),
            vmem((n_sib,) + top_coupling.shape, f32),
            vmem((leaf, 128), f32), vmem((tile, leaf), bf16), vmem((leaf, leaf), bf16),
            vmem((leaf, leaf), bf16), vmem((leaf, leaf), bf16)]
        + [vmem((leaf, rank), bf16)] * 6
        + [vmem((2 * rank, leaf), bf16)] * 2
        + [vmem((n_grp * rank, rank), bf16)] * 2
        + [vmem((leaf, cols), f32)] * 2 + [vmem((leaf, cols), bf16)] * 2 + [vmem((leaf, cols), f32)] * 2
        + [
            vmem((ITERS, rank, cols), f32), vmem((ITERS, n_sib, rank, cols), f32),
            vmem((ITERS, cols, rank), f32), vmem((ITERS, n_sib, part, rank), f32),
            vmem((ITERS, n_chip, 2, part, rank), f32), vmem((ITERS, cols, rank), f32),
            dma((7,)), dma((1 + leaf // tile,)), dma((n_sib,)), dma((n_sib,)),
            dma((ITERS, n_sib)), dma((ITERS, n_sib)), dma((ITERS, n_sib)), dma((ITERS, n_sib)),
            dma((ITERS, n_chip, 2)), dma((ITERS, n_chip, 2)), dma((ITERS, n_sib)), dma((ITERS, n_sib))],
        compiler_params=pltpu.CompilerParams(
            collective_id=0, has_side_effects=True, vmem_limit_bytes=56 * 1024 * 1024),
    )(targets, leaf_order, near_block, leaf_basis, sibling_coupling, transfer, top_coupling)
    fitted = jnp.tanh(field)
    coefficients = previous + step_size * (targets - fitted) - step_size * shrink_rate * previous
    return coefficients, fitted


def solution(mesh):
    spec = P(("grp", "sib"), None)
    return jax.shard_map(
        functools.partial(shards, mesh.shape["grp"], mesh.shape["sib"]),
        mesh=mesh,
        in_specs=(spec,) * 6 + (P("grp", "sib"),),
        out_specs=(spec, spec),
        check_vma=False,
    )
```

time: 201 us -> 64.5 us (0.32); the launches traced: 198 us -> 63.9 us
  blocking collectives: 60.7 us -> 0 us
  Pallas kernels: 0 us -> 59.7 us
  matrix products: 59.2 us -> 0 us
  local copies, waits for them, and re-layouts: 32.1 us -> 0.01 us
  waiting for transfers between devices: 28.5 us -> 0 us
  between operations: 14.2 us -> 0.66 us
    all_gather x5 -> x0, blocking collectives: 60.7 us -> none  [the longest x3 39 us: shards(): lax.all_gather(leaf_coefficients, 'sib', axis=0, tiled=True)]
    pallas_call x0 -> x1, Pallas kernels: none -> 59.7 us  [shards(): pl.pallas_call(functools.partial(kernel, n_grp, n_sib), out_shape=(jax.Sh...]
    dot_general x21 -> x0, matrix products: 59.2 us -> none  [matmul(): jnp.dot(left, right, precision=highest_level, preferred_element_type=jnp....]
    all_gather x3 -> x0, waiting for transfers between devices: 28.4 us -> none  [shards(): stacked = lax.all_gather(cluster_coefficient, 'grp', axis=0, tiled=True)]
    scatter x2 -> x0, local copies, waits for them, and re-layouts: 19.3 us -> none  [the longest x1 9.77 us: shards(): jnp.zeros_like(weight_coefficients).at[ordering].set(weight_coefficients)]
    gather x2 -> x0, local copies, waits for them, and re-layouts: 5.88 us -> none  [shards(): tree_targets = jnp.take(targets, ordering, axis=0)]
    sub x0 -> x1, other arithmetic: none -> 3.48 us  [shards(): previous + step_size * (targets - fitted)]
    sub x1 -> x0, local copies, waits for them, and re-layouts: 2.89 us -> none  [shards(): weight_coefficients + step_size * (tree_targets - fitted)]
  transfers between devices with their start and end apart: 3 -> 0, of which waited for: 3 -> 0; matrix products, arithmetic and copies ran while one was open for 15% -> 0% of each run, Pallas kernels for 0% -> 0%
where the time goes in v1:
time: 64.5 us; the launch traced here: 63.9 us
  Pallas kernels  59.7 us (93%)
  other arithmetic  3.48 us (5%)
  between operations  0.66 us (1%)
    pallas_call x1, Pallas kernels, shards(): pl.pallas_call(functools.partial(kernel, n_grp, n_sib), out_shape=(jax.Sh...  59.7 us
    sub x1, other arithmetic, shards(): previous + step_size * (targets - fitted)  3.48 us

profile of v1, /device:TPU:0, one launch (start us, length us, event | category | flops | bytes accessed | tf_op | source)
XLA Modules:
  0.0 63.9 jit_solution(15304953321561293104)
XLA Ops:
  0.6 0.0 copy-start
  0.6 59.7 %shard_map.86 = (f32[1280,256]{1,0:T(8,128)}, f32[1280,256]{1,0:T(8,128)}) custom-call(f32[1280,256]{1,0:T(8,128)} %targets.1, s32[1,1280]{1,0:T(1,128)} %order.1, f32[1280,1280]{1,0:T(8,128)} %near.1, f32[1280,128]{1,0:T(8,128)} %basis.1, f32[128,512]{1,0:T(8,128)} %sibling.1, f32[128,128]{1,0:T(8,128)} %transfer.1, f32[128,256]{1,0:T(8,128)} %top.1), custom_call_target="tpu_custom_call" | custom-call | tf_op jit(solution)/shard_map/pallas_call | solution.py:259
  60.4 0.0 copy-done
  60.4 3.5 %multiply_subtract_fusion = (f32[1280,256]{1,0:T(8,128)}, f32[1280,256]{1,0:T(8,128)}) fusion(f32[1280,256]{1,0:T(8,128)} %get-tuple-element.4, f32[1280,256]{1,0:T(8,128)S(1)} %copy-done, f32[1280,256]{1,0:T(8,128)} %get-tuple-element.5), kind=kLoop, calls=%fused_computation | loop fusion | flops 1638400 | bytes 6553600 | tf_op jit(solution)/shard_map/sub | solution.py:285
Async XLA Ops:
  0.6 59.8 %copy-start = (f32[1280,256]{1,0:T(8,128)S(1)}, f32[1280,256]{1,0:T(8,128)}, u32[]{:S(2)}) copy-start(f32[1280,256]{1,0:T(8,128)} %targets.1) | copy-start | bytes 3932164

commit v2 on v1

--- a/solution.py
+++ b/solution.py
@@ -31,7 +31,7 @@
 def kernel(n_grp, n_sib, targets, order, near, basis, sibling, transfer, top,
            prev_out, field_out,
            t_v, o_v, n_v, u_v, s_v, r_v, top_v,
-           oc_v, g_v, gt_v, nh_v, nl_v, uh_v, ul_v, wh_v, wl_v, ph_v, pl_v,
+           oc_v, g_v, gt_v, nh_v, nl_v, b_v, p_v,
            uwh_v, uwl_v, bh_v, bl_v, tt_v, x_v, xh_v, xl_v, pre_v, prev_v,
            c_own, c_all, d_own, d_sib, d_grp, z_all,
            load_sem, out_sem, top_send, top_recv, d_send, d_recv, c_send, c_recv,
@@ -89,11 +89,7 @@
     loads[2].wait()
     loads[3].wait()
 
-    th, tl = split(t_v[...])
-    xh_v[...] = th
-    tlow = tl
-    prev_v[...] = jnp.zeros_like(prev_v)
-    xl_v[...] = tlow
+    xh_v[...], xl_v[...] = split(t_v[...])
 
     def to_tree(r, i):
         own = oc_v[r, :]
@@ -119,8 +115,11 @@
 
     def second_basis(r, i):
         pair = split(u_v[r, :])
-        uh_v[r, :], ul_v[r, :] = pair
-        wh_v[r, :], wl_v[r, :] = split(dot3(pair, r_pair))
+        b_v[r, :rank], b_v[r, rank:2 * rank] = split(dot3(pair, r_pair))
+        b_v[r, 2 * rank:3 * rank], b_v[r, 3 * rank:] = pair
+
+    def times_basis(ref, r, at, pair, twice):
+        return dot(ref[r, at:at + 2 * rank], twice) + dot(ref[r, at:at + rank], pair[1])
 
     def near_first(r, i):
         pair = split(n_v[r, :])
@@ -133,8 +132,7 @@
     def to_data(r, i):
         q = lax.broadcasted_iota(jnp.int32, (tile, leaf), 0) + i * tile
         gt_v[r, :] = jnp.where(q == o_v[...], 1.0, 0.0).astype(bf16)
-        ph_v[r, :] = dot(gt_v[r, :], wh_v[...]).astype(bf16)
-        pl_v[r, :] = dot(gt_v[r, :], wl_v[...]).astype(bf16)
+        p_v[r, :] = dot(gt_v[r, :], b_v[...]).astype(bf16)
 
     for it in range(ITERS):
         final = it == ITERS - 1
@@ -143,13 +141,10 @@
         d_copies = [send(d_own.at[it, pl.ds(pl.multiple_of(sib_at(k) * part, part), part)], d_sib.at[it, k],
                          d_send.at[it, k], d_recv.at[it, k], (grp, sib_at(k))) for k in range(1, n_sib)]
         c_own[it] = both[:rank, :]
-        c_copies = [send(c_own.at[it], c_all.at[it, k], c_send.at[it, k], c_recv.at[it, k],
-                         (grp, sib_at(k))) for k in range(1, n_sib)]
         if it == 0:
-            over_tiles(0, tiles, second_basis)
             loads[4].wait()
         near_part = near_first if it == 0 else near_again
-        early = (tiles + 1) // 2 if it == 0 else tiles
+        early = (tiles + 1) // 2 if it == 0 else max(tiles - 1, 1)
         over_tiles(0, early, near_part)
 
         total = d_own[it, pl.ds(pl.multiple_of(sib * part, part), part), :]
@@ -162,8 +157,12 @@
                          (chip_at(k) * 2 + core, sib)) for k in range(1, n_chip)]
         relays = [send(mine, d_grp.at[it, 0, 1], g_send.at[it, 0, 1], g_recv.at[it, 0, 1], partner)]
 
+        c_copies = [send(c_own.at[it], c_all.at[it, k], c_send.at[it, k], c_recv.at[it, k],
+                         (grp, sib_at(k))) for k in range(1, n_sib)]
+
         over_tiles(early, tiles, near_part)
         if it == 0:
+            over_tiles(0, tiles, second_basis)
             for copy in top_copies:
                 copy.wait_recv()
             loads[5].wait()
@@ -178,6 +177,15 @@
             over_tiles(0, tiles, prev_to_data)
             out_prev = pltpu.make_async_copy(prev_v, prev_out, out_sem.at[0])
             out_prev.start()
+
+            def pre_split(r, i):
+                xh_v[r, :], xl_v[r, :] = split(pre_v[r, :])
+
+            def pre_to_data(r, i):
+                pre_v[r, :] = dot(gt_v[r, :], xh_v[...]) + dot(gt_v[r, :], xl_v[...])
+
+            over_tiles(0, tiles, pre_split)
+            over_tiles(0, tiles, pre_to_data)
 
         def from_group(k, other):
             group = chip_at(-k) * 2 + (1 - core if other else core)
@@ -206,40 +214,36 @@
             block = s_v[:, pl.ds(pl.multiple_of(sib_at(-k) * rank, rank), rank)]
             down = down + dot3(split(block), split(c_all[it, k]))
         down_pair = split(down)
+        down_twice = jnp.concatenate([down_pair[0]] * 2, axis=0)
+        basis_v = p_v if final else b_v
 
         def add_siblings(r, i):
-            pre_v[r, :] = pre_v[r, :] + dot3((uh_v[r, :], ul_v[r, :]), down_pair)
-
-        over_tiles(0, tiles, add_siblings)
-        if final:
-            def pre_split(r, i):
-                xh_v[r, :], xl_v[r, :] = split(pre_v[r, :])
-
-            def pre_to_data(r, i):
-                pre_v[r, :] = dot(gt_v[r, :], xh_v[...]) + dot(gt_v[r, :], xl_v[...])
-
-            over_tiles(0, tiles, pre_split)
-            over_tiles(0, tiles, pre_to_data)
+            pre_v[r, :] = pre_v[r, :] + times_basis(basis_v, r, 2 * rank, down_pair, down_twice)
+
+        for i in range(tiles):
+            add_siblings(pl.ds(i * tile, tile), i)
 
         for copy in z_copies:
             copy.wait_recv()
         z_pair = split(z_all[it].T)
+        z_twice = jnp.concatenate([z_pair[0]] * 2, axis=0)
         if final:
             outs = []
             for i in range(tiles):
                 r = pl.ds(i * tile, tile)
-                pre_v[r, :] = pre_v[r, :] + dot3((ph_v[r, :], pl_v[r, :]), z_pair)
+                pre_v[r, :] = pre_v[r, :] + times_basis(p_v, r, 0, z_pair, z_twice)
                 outs.append(pltpu.make_async_copy(pre_v.at[r], field_out.at[r], out_sem.at[1 + i]))
                 outs[-1].start()
         else:
             def update(r, i):
-                fitted = jnp.tanh(pre_v[r, :] + dot3((wh_v[r, :], wl_v[r, :]), z_pair))
+                fitted = jnp.tanh(pre_v[r, :] + times_basis(b_v, r, 0, z_pair, z_twice))
                 old = x_v[r, :]
                 new = old + step_size * (tt_v[r, :] - fitted) - step_size * shrink_rate * old
                 x_v[r, :] = new
                 xh_v[r, :], xl_v[r, :] = split(new)
 
-            over_tiles(0, tiles, update)
+            for i in range(tiles):
+                update(pl.ds(i * tile, tile), i)
 
     for copy in pending:
         copy.wait_send()
@@ -267,7 +271,7 @@
             vmem((n_sib,) + top_coupling.shape, f32),
             vmem((leaf, 128), f32), vmem((tile, leaf), bf16), vmem((leaf, leaf), bf16),
             vmem((leaf, leaf), bf16), vmem((leaf, leaf), bf16)]
-        + [vmem((leaf, rank), bf16)] * 6
+        + [vmem((leaf, 4 * rank), bf16)] * 2
         + [vmem((2 * rank, leaf), bf16)] * 2
         + [vmem((n_grp * rank, rank), bf16)] * 2
         + [vmem((leaf, cols), f32)] * 2 + [vmem((leaf, cols), bf16)] * 2 + [vmem((leaf, cols), f32)] * 2

time: 64.5 us -> 61.4 us (0.952)
  Pallas kernels: 59.7 us -> 57.1 us
    pallas_call x1, Pallas kernels: 59.7 us -> 57.1 us  [shards(): pl.pallas_call(functools.partial(kernel, n_grp, n_sib), out_shape=(jax.Sh...]
where the time goes in v2:
time: 61.4 us; the launch traced here: 61.2 us
  Pallas kernels  57.1 us (93%)
  other arithmetic  3.48 us (6%)
  between operations  0.66 us (1%)
    pallas_call x1, Pallas kernels, shards(): pl.pallas_call(functools.partial(kernel, n_grp, n_sib), out_shape=(jax.Sh...  57.1 us
    sub x1, other arithmetic, shards(): previous + step_size * (targets - fitted)  3.48 us

profile of v2, /device:TPU:0, one launch (start us, length us, event | category | flops | bytes accessed | tf_op | source)
XLA Modules:
  0.0 61.2 jit_solution(2831161866932723776)
XLA Ops:
  0.6 0.0 copy-start
  0.6 57.1 %shard_map.86 = (f32[1280,256]{1,0:T(8,128)}, f32[1280,256]{1,0:T(8,128)}) custom-call(f32[1280,256]{1,0:T(8,128)} %targets.1, s32[1,1280]{1,0:T(1,128)} %order.1, f32[1280,1280]{1,0:T(8,128)} %near.1, f32[1280,128]{1,0:T(8,128)} %basis.1, f32[128,512]{1,0:T(8,128)} %sibling.1, f32[128,128]{1,0:T(8,128)} %transfer.1, f32[128,256]{1,0:T(8,128)} %top.1), custom_call_target="tpu_custom_call" | custom-call | tf_op jit(solution)/shard_map/pallas_call | solution.py:263
  57.8 0.0 copy-done
  57.8 3.5 %multiply_subtract_fusion = (f32[1280,256]{1,0:T(8,128)}, f32[1280,256]{1,0:T(8,128)}) fusion(f32[1280,256]{1,0:T(8,128)} %get-tuple-element.4, f32[1280,256]{1,0:T(8,128)S(1)} %copy-done, f32[1280,256]{1,0:T(8,128)} %get-tuple-element.5), kind=kLoop, calls=%fused_computation | loop fusion | flops 1638400 | bytes 6553600 | tf_op jit(solution)/shard_map/sub | solution.py:289
Async XLA Ops:
  0.6 57.1 %copy-start = (f32[1280,256]{1,0:T(8,128)S(1)}, f32[1280,256]{1,0:T(8,128)}, u32[]{:S(2)}) copy-start(f32[1280,256]{1,0:T(8,128)} %targets.1) | copy-start | bytes 3932164
